TPU v7x, 32 devices: a whole 2x2x4 slice. The times are simulated.
32 devices in a mesh: patch: 16 (over z, x, core), lev: 2 (over y).
Axes of the slice: x: 2, y: 2, z: 4, core: 2. Of those that a mesh axis runs over, the one named last changes fastest.
Arguments:
- fields: bfloat16 [8, 32, 32768], P(None, 'lev', 'patch'), may hold values from -6 to 6
- interp: bfloat16 [128, 128, 256], P('patch'), may hold values from -0.375 to 0.375
- conv_weight: bfloat16 [128, 8, 128, 128], P('patch'), may hold values from -0.1875 to 0.1875
- vert_weight: float32 [32, 5], replicated, may hold values from 0.1 to 0.5
- send_tiles: int32 [16, 4, 2], P('patch'), may hold values from 0 to 8, as said below
- tile_pattern: int32 [128, 8], P('patch'), may hold values from 0 to 15, as said below
Outputs:
- localized: float32 [8, 32, 32768], P(None, 'lev', 'patch')
Inputs may be any that keep to these rules, and one draw needn't show every extreme that they name: `send_tiles`: in every draw some link carries 2 tiles; every link carries at least one tile; the tiles of one link are distinct. `tile_pattern`: each row names distinct entries, each an own tile or a filled received slot.
All inputs are finite; a program needn't handle non-finite values.
Results may differ from a plain program's by a relative error of at most 0.0048.
Values may be sent and summed in bfloat16 or wider, within the bound.
A program may use at most 64 MiB of HBM per device.

v0:
```python
import jax
import jax.numpy as jnp
from jax import lax
from jax.sharding import PartitionSpec as P

HIGHEST = lax.Precision.HIGHEST


def passed_along(block, axis, distance):
    devices = range(lax.axis_size(axis))
    route = [((i - distance) % len(devices), i) for i in devices]
    return lax.ppermute(block, axis, route)


def padded(block, sides, width):
    for axis, dim in sides:
        count = lax.axis_size(axis)
        forward = [(i, i + 1) for i in range(count - 1)]
        backward = [(target, source) for source, target in forward]
        low = lax.ppermute(
            lax.slice_in_dim(block, block.shape[dim] - width, None, axis=dim), axis, forward
        )
        high = lax.ppermute(lax.slice_in_dim(block, 0, width, axis=dim), axis, backward)
        block = jnp.concatenate([low, block, high], axis=dim)
    return block


def link_offsets(reach_len):
    return [
        position - reach_len if position < reach_len else position - reach_len + 1
        for position in range(2 * reach_len)
    ]


def vertical_adjoint(values, weights, length, half_width):
    summed = jnp.zeros(values.shape[:-2] + (length, values.shape[-1]), jnp.float32)
    for offset in range(-half_width, half_width + 1):
        factor = weights[half_width + offset : half_width + offset + length, half_width - offset]
        summed = summed + factor[:, None] * values[
            ..., half_width + offset : half_width + offset + length, :
        ].astype(jnp.float32)
    return summed


def vertical_forward(values, weights, length, half_width):
    summed = jnp.zeros(values.shape[:-2] + (length, values.shape[-1]), jnp.float32)
    for offset in range(2 * half_width + 1):
        factor = weights[half_width : half_width + length, offset]
        summed = summed + factor[:, None] * values[..., offset : offset + length, :].astype(
            jnp.float32
        )
    return summed


def move_links(pieces, reach_len, offsets, backward):
    if backward:
        return jnp.stack(
            [
                passed_along(pieces[position], "patch", -offsets[position])
                for position in range(2 * reach_len)
            ]
        )
    return jnp.stack(
        [
            passed_along(pieces[position], "patch", offsets[position])
            for position in range(2 * reach_len)
        ]
    )


def shards(fields, interp, conv_weight, vert_weight, send_tiles, tile_pattern):
    members, level_len, column_len = fields.shape
    tile_count, tile_len, fine_len = interp.shape
    reach_len = send_tiles.shape[1] // 2
    slot_most = send_tiles.shape[2]
    half_width = (vert_weight.shape[1] - 1) // 2
    row_count = members * level_len
    extended_len = tile_count + 2 * reach_len * slot_most
    offsets = link_offsets(reach_len)
    coarse = jnp.einsum(
        "rtf,tcf->trc",
        fields.reshape(row_count, tile_count, fine_len),
        interp,
        preferred_element_type=jnp.float32,
    ).astype(jnp.bfloat16)
    chosen = tile_pattern[:, :, None] == jnp.arange(extended_len, dtype=jnp.int32)[None, None, :]
    sending = (
        send_tiles[0][:, :, None] == jnp.arange(tile_count, dtype=jnp.int32)[None, None, :]
    ).astype(jnp.bfloat16)
    products = jnp.einsum("tro,tkio->tkri", coarse, conv_weight, preferred_element_type=jnp.float32)
    summed = jnp.einsum("tke,tkri->eri", chosen.astype(jnp.float32), products, precision=HIGHEST)
    own_part = summed[:tile_count]
    returning = (
        summed[tile_count:]
        .reshape(2 * reach_len, slot_most, row_count, tile_len)
        .astype(jnp.bfloat16)
    )
    arrived_back = move_links(returning, reach_len, offsets, True)
    added = jnp.einsum("ost,osri->tri", sending, arrived_back, preferred_element_type=jnp.float32)
    adjoint = (
        (own_part + added).astype(jnp.bfloat16).reshape(tile_count, members, level_len, tile_len)
    )
    start = lax.axis_index("lev") * level_len
    padded_weights = jnp.pad(vert_weight, ((2 * half_width, 2 * half_width), (0, 0)))
    window = lax.dynamic_slice_in_dim(padded_weights, start, level_len + 4 * half_width, 0)
    inner = window[half_width : half_width + level_len + 2 * half_width]
    widened = padded(adjoint, (("lev", 2),), 2 * half_width)
    middle = vertical_adjoint(widened, window, level_len + 2 * half_width, half_width)
    level_ids = start - half_width + jnp.arange(level_len + 2 * half_width, dtype=jnp.int32)
    inside = (level_ids >= 0) & (level_ids < vert_weight.shape[0])
    middle = jnp.where(inside[:, None], middle, 0.0).astype(jnp.bfloat16)
    smoothed = vertical_forward(middle, inner, level_len, half_width)
    smooth = smoothed.astype(jnp.bfloat16).reshape(tile_count, row_count, tile_len)
    slots = jnp.einsum("ost,tri->osri", sending, smooth, preferred_element_type=jnp.float32).astype(
        jnp.bfloat16
    )
    arrived = move_links(slots, reach_len, offsets, False)
    extended = jnp.concatenate([smooth, arrived.reshape(-1, row_count, tile_len)], axis=0)
    picked = jnp.einsum(
        "tke,eri->tkri", chosen.astype(jnp.bfloat16), extended, preferred_element_type=jnp.float32
    ).astype(jnp.bfloat16)
    mixed = jnp.einsum(
        "tkri,tkio->tro", picked, conv_weight, preferred_element_type=jnp.float32
    ).astype(jnp.bfloat16)
    result = jnp.einsum("tro,tof->rtf", mixed, interp, preferred_element_type=jnp.float32)
    return result.reshape(members, level_len, column_len)


def solution(mesh):
    in_specs = (
        P(None, "lev", "patch"),
        P("patch", None, None),
        P("patch", None, None, None),
        P(),
        P("patch", None, None),
        P("patch", None),
    )
    out_specs = P(None, "lev", "patch")
    return jax.shard_map(shards, mesh=mesh, in_specs=in_specs, out_specs=out_specs, check_vma=False)
```

profile of v0, /device:TPU:0, one launch (start us, length us, event | category | flops | bytes accessed | tf_op | source)
XLA Modules:
  0.0 57.8 jit_solution(4915136279785751203)
XLA Ops:
  0.0 0.0 copy-start
  0.0 0.9 %copy.34 = s32[8,8]{0,1:T(8,128)S(1)} copy(s32[8,8]{1,0:T(8,128)} %param.11) | data formatting | bytes 512 | tf_op args[5]
  0.9 1.1 %copy.51 = bf16[16,8,8,256]{3,2,1,0:T(8,128)(2,1)S(1)} copy(bf16[16,8,8,256]{3,1,2,0:T(8,128)(2,1)} %bitcast.107) | data formatting | bytes 1048576
  2.1 0.0 copy-done
  2.1 3.9 %convolution_bitcast_fusion = f32[8,8,128,128]{3,2,1,0:T(8,128)} fusion(bf16[8,8,128,128]{3,2,1,0:T(8,128)(2,1)S(1)} %copy-done, bf16[8,128,256]{2,1,0:T(8,128)(2,1)} %param.7, bf16[128,8,256]{2,1,0:T(8,128)(2,1)S(1)} %bitcast.105), kind=kOutput, calls=%fused_computation.2 | convolution fusion | flops 335675392 | bytes 7340032 | tf_op jit(solution)/shard_map/tro,tkio->tkri/dot_general | solution.py:90
  5.9 5.9 %fusion.39 = (bf16[16,128,128]{2,0,1:T(8,128)(2,1)S(1)}, f32[16,128,128]{2,0,1:T(8,128)S(1)}) fusion(f32[8,8,128,128]{3,2,1,0:T(8,128)} %convolution_bitcast_fusion, s32[8,8]{0,1:T(8,128)S(1)} %copy.34), kind=kOutput, calls=%fused_computation.56 | convolution fusion | flops 201589760 | bytes 5767424 | tf_op jit(solution)/shard_map/tke,tkri->eri/dot_general | solution.py:91
  11.8 0.8 %fusion.36 = (bf16[2,128,128]{2,0,1:T(2,128)(2,1)}, bf16[2,128,128]{2,0,1:T(2,128)(2,1)S(1)}, bf16[2,128,128]{2,0,1:T(2,128)(2,1)S(1)}, bf16[2,128,128]{2,0,1:T(2,128)(2,1)S(1)}) fusion(bf16[16,128,128]{2,0,1:T(8,128)(2,1)S(1)} %get-tuple-element.25), kind=kLoop, calls=%fused_computation.53 | loop fusion | bytes 524288 | tf_op jit(solution)/shard_map/slice | solution.py:59
  12.6 3.0 %collective-permute-start = (bf16[2,128,128]{2,0,1:T(2,128)(2,1)}, bf16[2,128,128]{2,0,1:T(2,128)(2,1)S(1)}, u32[]{:S(2)}, u32[]{:S(2)}) collective-permute-start(bf16[2,128,128]{2,0,1:T(2,128)(2,1)} %get-tuple-element.5), channel_id=1, source_target_pairs={{28,0},{30,2},{0,4},{2,6},{4,8},{6,10},{8,12},{10,14},{12,16},{14,... | collective-permute-start | bytes 196616 | tf_op jit(solution)/shard_map/ppermute | solution.py:12
  15.6 0.0 collective-permute-start.1
  15.6 4.4 %collective-permute-start.2 = (bf16[2,128,128]{2,0,1:T(2,128)(2,1)S(1)}, bf16[2,128,128]{2,0,1:T(2,128)(2,1)S(1)}, u32[]{:S(2)}, u32[]{:S(2)}) collective-permute-start(bf16[2,128,128]{2,0,1:T(2,128)(2,1)S(1)} %get-tuple-element.7), channel_id=1, source_target_pairs={{2,0},{4,2},{6,4},{8,6},{10,8},{12,10},{14,12},{16,14},{18,16},{20... | collective-permute-start | bytes 196616 | tf_op jit(solution)/shard_map/ppermute | solution.py:12
  20.0 0.3 collective-permute-start.3
  20.4 0.0 copy-done.3
  20.4 0.1 pad_dynamic-slice_fusion
  20.5 0.7 %slice_bitcast_fusion.8 = (f32[20]{0:T(128)}, f32[20]{0:T(128)}, f32[20]{0:T(128)}, f32[20]{0:T(128)}, f32[20]{0:T(128)}) fusion(f32[24,5]{0,1:T(8,128)S(1)} %pad_dynamic-slice_fusion), kind=kLoop, calls=%fused_computation.50 | loop fusion | bytes 800 | tf_op jit(solution)/shard_map/mul | solution.py:39
  21.1 0.7 %slice_bitcast_fusion.9 = (f32[16]{0:T(128)S(1)}, f32[16]{0:T(128)S(1)}, f32[16]{0:T(128)}, f32[16]{0:T(128)}, f32[16]{0:T(128)}) fusion(f32[24,5]{0,1:T(8,128)S(1)} %pad_dynamic-slice_fusion), kind=kLoop, calls=%fused_computation.51 | loop fusion | bytes 640 | tf_op jit(solution)/shard_map/mul | solution.py:49
  21.8 0.0 copy-start.11
  21.8 0.0 collective-permute-done
  21.8 0.2 collective-permute-done.1
  22.0 0.0 collective-permute-done.2
  22.0 2.4 %collective-permute-done.3 = bf16[2,128,128]{2,0,1:T(2,128)(2,1)} collective-permute-done((bf16[2,128,128]{2,0,1:T(2,128)(2,1)S(1)}, bf16[2,128,128]{2,0,1:T(2,128)(2,1)}, u32[]{:S(2)}, u32[]{:S(2)}) %collective-permute-start.3) | collective-permute-done | bytes 65568 | tf_op jit(solution)/shard_map/ppermute | solution.py:12
  24.4 1.3 %pad_maximum_fusion.1 = bf16[4,2,128,128]{3,1,2,0:T(2,128)(2,1)S(1)} fusion(bf16[1,2,128,128]{3,1,2,0:T(2,128)(2,1)} %bitcast.14, bf16[1,2,128,128]{3,1,2,0:T(2,128)(2,1)S(1)} %bitcast.114, bf16[1,2,128,128]{3,1,2,0:T(2,128)(2,1)S(1)} %bitcast.113, bf16[1,2,128,128]{3,1,2,0:T(2,128)(2,1)S(1)} %bitcast.112), kind=kLoop, calls=%fused_computation.23 | loop fusion | flops 393216 | bytes 524288 | tf_op jit(solution)/shard_map/stack | solution.py:57
  25.7 0.5 fusion.11
  26.3 3.4 %collective-permute-start.4 = (bf16[8,8,4,128]{3,0,2,1:T(8,128)(2,1)S(1)}, bf16[8,8,4,128]{3,0,2,1:T(8,128)(2,1)S(1)}, u32[]{:S(2)}, u32[]{:S(2)}) collective-permute-start(bf16[8,8,4,128]{3,0,2,1:T(8,128)(2,1)S(1)} %get-tuple-element.13), channel_id=1, source_target_pairs={{0,1},{2,3},{4,5},{6,7},{8,9},{10,11},{12,13},{14,15},{16,17},{18,... | collective-permute-start | bytes 196616 | tf_op jit(solution)/shard_map/ppermute | solution.py:20
  29.7 1.3 %collective-permute-start.5 = (bf16[8,8,4,128]{3,0,2,1:T(8,128)(2,1)S(1)}, bf16[8,8,4,128]{3,0,2,1:T(8,128)(2,1)S(1)}, u32[]{:S(2)}, u32[]{:S(2)}) collective-permute-start(bf16[8,8,4,128]{3,0,2,1:T(8,128)(2,1)S(1)} %get-tuple-element.14), channel_id=1, source_target_pairs={{1,0},{3,2},{5,4},{7,6},{9,8},{11,10},{13,12},{15,14},{17,16},{19,... | collective-permute-start | bytes 196616 | tf_op jit(solution)/shard_map/ppermute | solution.py:23
  31.0 0.6 collective-permute-done.4
  31.6 4.3 %collective-permute-done.5 = bf16[8,8,4,128]{3,0,2,1:T(8,128)(2,1)S(1)} collective-permute-done((bf16[8,8,4,128]{3,0,2,1:T(8,128)(2,1)S(1)}, bf16[8,8,4,128]{3,0,2,1:T(8,128)(2,1)S(1)}, u32[]{:S(2)}, u32[]{:S(2)}) %collective-permute-start.5) | collective-permute-done | bytes 65568 | tf_op jit(solution)/shard_map/ppermute | solution.py:23
  35.9 0.0 copy-done.7
  35.9 0.0 copy-done.8
  35.9 0.0 copy-done.9
  35.9 0.0 copy-done.10
  35.9 0.0 copy-done.11
  36.0 0.4 select_convert_fusion
  36.4 0.3 add_convert_fusion
  36.8 0.3 convolution_convert_fusion.1
  37.1 0.4 fusion.37
  37.5 3.6 %collective-permute-start.6 = (bf16[2,128,128]{2,1,0:T(8,128)(2,1)S(1)}, bf16[2,128,128]{2,1,0:T(8,128)(2,1)S(1)}, u32[]{:S(2)}, u32[]{:S(2)}) collective-permute-start(bf16[2,128,128]{2,1,0:T(8,128)(2,1)S(1)} %bitcast.108), channel_id=1, source_target_pairs={{4,0},{6,2},{8,4},{10,6},{12,8},{14,10},{16,12},{18,14},{20,16},{2... | collective-permute-start | bytes 196616 | tf_op jit(solution)/shard_map/ppermute | solution.py:12
  41.1 0.1 collective-permute-start.7
  41.2 0.5 collective-permute-start.8
  41.7 0.1 collective-permute-start.9
  41.8 1.2 %collective-permute-done.6 = bf16[2,128,128]{2,1,0:T(8,128)(2,1)S(1)} collective-permute-done((bf16[2,128,128]{2,1,0:T(8,128)(2,1)S(1)}, bf16[2,128,128]{2,1,0:T(8,128)(2,1)S(1)}, u32[]{:S(2)}, u32[]{:S(2)}) %collective-permute-start.6) | collective-permute-done | bytes 65568 | tf_op jit(solution)/shard_map/ppermute | solution.py:12
  43.0 0.6 %collective-permute-done.7 = bf16[2,128,128]{2,1,0:T(8,128)(2,1)S(1)} collective-permute-done((bf16[2,128,128]{2,1,0:T(8,128)(2,1)S(1)}, bf16[2,128,128]{2,1,0:T(8,128)(2,1)S(1)}, u32[]{:S(2)}, u32[]{:S(2)}) %collective-permute-start.7) | collective-permute-done | bytes 65568 | tf_op jit(solution)/shard_map/ppermute | solution.py:12
  43.6 4.0 %collective-permute-done.8 = bf16[2,128,128]{2,1,0:T(8,128)(2,1)S(1)} collective-permute-done((bf16[2,128,128]{2,1,0:T(8,128)(2,1)S(1)}, bf16[2,128,128]{2,1,0:T(8,128)(2,1)S(1)}, u32[]{:S(2)}, u32[]{:S(2)}) %collective-permute-start.8) | collective-permute-done | bytes 65568 | tf_op jit(solution)/shard_map/ppermute | solution.py:12
  47.6 1.4 %collective-permute-done.9 = bf16[2,128,128]{2,1,0:T(8,128)(2,1)S(1)} collective-permute-done((bf16[2,128,128]{2,1,0:T(8,128)(2,1)S(1)}, bf16[2,128,128]{2,1,0:T(8,128)(2,1)S(1)}, u32[]{:S(2)}, u32[]{:S(2)}) %collective-permute-start.9) | collective-permute-done | bytes 65568 | tf_op jit(solution)/shard_map/ppermute | solution.py:12
  49.0 0.3 copy.38
  49.3 2.1 %convolution_convert_fusion = bf16[8,8,128,128]{3,0,2,1:T(8,128)(2,1)} fusion(bf16[8,128,128]{2,0,1:T(8,128)(2,1)S(1)} %bitcast.106, bf16[8,128,128]{2,0,1:T(8,128)(2,1)S(1)} %bitcast.104, s32[8,8]{0,1:T(8,128)S(1)} %copy.34), kind=kOutput, calls=%fused_computation.5 | convolution fusion | flops 35652608 | bytes 2621696 | tf_op jit(solution)/shard_map/tke,eri->tkri/dot_general | solution.py:119
  51.4 3.5 %convolution_bitcast_fusion.1 = f32[128,8,256]{2,0,1:T(8,128)} fusion(bf16[8,128,256]{2,1,0:T(8,128)(2,1)S(1)} %copy-done.1, bf16[8,8,128,128]{3,2,1,0:T(8,128)(2,1)S(1)} %copy-done, bf16[8,8,128,128]{3,0,2,1:T(8,128)(2,1)} %convolution_convert_fusion), kind=kOutput, calls=%fused_computation.7 | convolution fusion | flops 335675392 | bytes 5767168 | tf_op jit(solution)/shard_map/tro,tof->rtf/dot_general | solution.py:125
  54.9 1.8 %copy.40 = f32[128,8,256]{2,1,0:T(8,128)S(1)} copy(f32[128,8,256]{2,0,1:T(8,128)} %convolution_bitcast_fusion.1) | data formatting | bytes 2097152 | tf_op jit(solution)/shard_map/tro,tof->rtf/transpose | solution.py:125
  56.7 1.1 %reshape.41 = f32[8,16,2048]{2,1,0:T(8,128)} reshape(f32[128,8,256]{2,1,0:T(8,128)S(1)} %copy.40) | data formatting | bytes 2097152 | tf_op jit(solution)/shard_map/reshape | solution.py:126
  (23 shorter events, 0.2 us)
Async XLA Ops:
  0.0 2.1 %copy-start = (bf16[8,8,128,128]{3,2,1,0:T(8,128)(2,1)S(1)}, bf16[8,8,128,128]{3,2,1,0:T(8,128)(2,1)}, u32[]{:S(2)}) copy-start(bf16[8,8,128,128]{3,2,1,0:T(8,128)(2,1)} %param.8) | copy-start | bytes 6291460
  5.9 14.4 %copy-start.3 = (f32[32,5]{0,1:T(8,128)S(1)}, f32[32,5]{0,1:T(8,128)}, u32[]{:S(2)}) copy-start(f32[32,5]{0,1:T(8,128)} %param.9) | copy-start | bytes 1924
  5.9 19.8 %copy-start.2 = (s32[1,4,2]{1,2,0:T(2,128)S(1)}, s32[1,4,2]{1,2,0:T(2,128)}, u32[]{:S(2)}) copy-start(s32[1,4,2]{1,2,0:T(2,128)} %param.10) | copy-start | bytes 100
  12.6 9.2 %collective-permute-start = (bf16[2,128,128]{2,0,1:T(2,128)(2,1)}, bf16[2,128,128]{2,0,1:T(2,128)(2,1)S(1)}, u32[]{:S(2)}, u32[]{:S(2)}) collective-permute-start(bf16[2,128,128]{2,0,1:T(2,128)(2,1)} %get-tuple-element.5), channel_id=1, source_target_pairs={{28,0},{30,2},{0,4},{2,6},{4,8},{6,10},{8,12},{10,14},{12,16},{14,... | collective-permute-start | bytes 196616 | tf_op jit(solution)/shard_map/ppermute | solution.py:12
  15.6 6.4 %collective-permute-start.1 = (bf16[2,128,128]{2,0,1:T(2,128)(2,1)S(1)}, bf16[2,128,128]{2,0,1:T(2,128)(2,1)S(1)}, u32[]{:S(2)}, u32[]{:S(2)}) collective-permute-start(bf16[2,128,128]{2,0,1:T(2,128)(2,1)S(1)} %get-tuple-element.8), channel_id=1, source_target_pairs={{30,0},{0,2},{2,4},{4,6},{6,8},{8,10},{10,12},{12,14},{14,16},{16,... | collective-permute-start | bytes 196616 | tf_op jit(solution)/shard_map/ppermute | solution.py:12
  15.6 6.4 %collective-permute-start.2 = (bf16[2,128,128]{2,0,1:T(2,128)(2,1)S(1)}, bf16[2,128,128]{2,0,1:T(2,128)(2,1)S(1)}, u32[]{:S(2)}, u32[]{:S(2)}) collective-permute-start(bf16[2,128,128]{2,0,1:T(2,128)(2,1)S(1)} %get-tuple-element.7), channel_id=1, source_target_pairs={{2,0},{4,2},{6,4},{8,6},{10,8},{12,10},{14,12},{16,14},{18,16},{20... | collective-permute-start | bytes 196616 | tf_op jit(solution)/shard_map/ppermute | solution.py:12
  20.0 4.4 %collective-permute-start.3 = (bf16[2,128,128]{2,0,1:T(2,128)(2,1)S(1)}, bf16[2,128,128]{2,0,1:T(2,128)(2,1)}, u32[]{:S(2)}, u32[]{:S(2)}) collective-permute-start(bf16[2,128,128]{2,0,1:T(2,128)(2,1)S(1)} %get-tuple-element.6), channel_id=1, source_target_pairs={{4,0},{6,2},{8,4},{10,6},{12,8},{14,10},{16,12},{18,14},{20,16},{2... | collective-permute-start | bytes 196616 | tf_op jit(solution)/shard_map/ppermute | solution.py:12
  21.8 14.1 %copy-start.7 = (f32[20]{0:T(128)S(1)}, f32[20]{0:T(128)}, u32[]{:S(2)}) copy-start(f32[20]{0:T(128)} %get-tuple-element.20) | copy-start | bytes 244
  21.8 14.1 %copy-start.8 = (f32[20]{0:T(128)S(1)}, f32[20]{0:T(128)}, u32[]{:S(2)}) copy-start(f32[20]{0:T(128)} %get-tuple-element.21) | copy-start | bytes 244
  21.8 14.1 %copy-start.9 = (f32[20]{0:T(128)S(1)}, f32[20]{0:T(128)}, u32[]{:S(2)}) copy-start(f32[20]{0:T(128)} %get-tuple-element.22) | copy-start | bytes 244
  21.8 14.2 %copy-start.10 = (f32[20]{0:T(128)S(1)}, f32[20]{0:T(128)}, u32[]{:S(2)}) copy-start(f32[20]{0:T(128)} %get-tuple-element.23) | copy-start | bytes 244
  21.8 14.2 %copy-start.11 = (f32[20]{0:T(128)S(1)}, f32[20]{0:T(128)}, u32[]{:S(2)}) copy-start(f32[20]{0:T(128)} %get-tuple-element.24) | copy-start | bytes 244
  24.4 12.0 %copy-start.4 = (f32[16]{0:T(128)S(1)}, f32[16]{0:T(128)}, u32[]{:S(2)}) copy-start(f32[16]{0:T(128)} %get-tuple-element.17) | copy-start | bytes 196
  24.4 12.0 %copy-start.5 = (f32[16]{0:T(128)S(1)}, f32[16]{0:T(128)}, u32[]{:S(2)}) copy-start(f32[16]{0:T(128)} %get-tuple-element.18) | copy-start | bytes 196
  24.4 12.0 %copy-start.6 = (f32[16]{0:T(128)S(1)}, f32[16]{0:T(128)}, u32[]{:S(2)}) copy-start(f32[16]{0:T(128)} %get-tuple-element.19) | copy-start | bytes 196
  26.3 5.3 %collective-permute-start.4 = (bf16[8,8,4,128]{3,0,2,1:T(8,128)(2,1)S(1)}, bf16[8,8,4,128]{3,0,2,1:T(8,128)(2,1)S(1)}, u32[]{:S(2)}, u32[]{:S(2)}) collective-permute-start(bf16[8,8,4,128]{3,0,2,1:T(8,128)(2,1)S(1)} %get-tuple-element.13), channel_id=1, source_target_pairs={{0,1},{2,3},{4,5},{6,7},{8,9},{10,11},{12,13},{14,15},{16,17},{18,... | collective-permute-start | bytes 196616 | tf_op jit(solution)/shard_map/ppermute | solution.py:20
  29.7 6.2 %collective-permute-start.5 = (bf16[8,8,4,128]{3,0,2,1:T(8,128)(2,1)S(1)}, bf16[8,8,4,128]{3,0,2,1:T(8,128)(2,1)S(1)}, u32[]{:S(2)}, u32[]{:S(2)}) collective-permute-start(bf16[8,8,4,128]{3,0,2,1:T(8,128)(2,1)S(1)} %get-tuple-element.14), channel_id=1, source_target_pairs={{1,0},{3,2},{5,4},{7,6},{9,8},{11,10},{13,12},{15,14},{17,16},{19,... | collective-permute-start | bytes 196616 | tf_op jit(solution)/shard_map/ppermute | solution.py:23
  37.5 5.5 %collective-permute-start.6 = (bf16[2,128,128]{2,1,0:T(8,128)(2,1)S(1)}, bf16[2,128,128]{2,1,0:T(8,128)(2,1)S(1)}, u32[]{:S(2)}, u32[]{:S(2)}) collective-permute-start(bf16[2,128,128]{2,1,0:T(8,128)(2,1)S(1)} %bitcast.108), channel_id=1, source_target_pairs={{4,0},{6,2},{8,4},{10,6},{12,8},{14,10},{16,12},{18,14},{20,16},{2... | collective-permute-start | bytes 196616 | tf_op jit(solution)/shard_map/ppermute | solution.py:12
  41.1 10.3 %copy-start.1 = (bf16[8,128,256]{2,1,0:T(8,128)(2,1)S(1)}, bf16[8,128,256]{2,1,0:T(8,128)(2,1)}, u32[]{:S(2)}) copy-start(bf16[8,128,256]{2,1,0:T(8,128)(2,1)} %param.7) | copy-start | bytes 1572868
  41.1 2.5 %collective-permute-start.7 = (bf16[2,128,128]{2,1,0:T(8,128)(2,1)S(1)}, bf16[2,128,128]{2,1,0:T(8,128)(2,1)S(1)}, u32[]{:S(2)}, u32[]{:S(2)}) collective-permute-start(bf16[2,128,128]{2,1,0:T(8,128)(2,1)S(1)} %bitcast.109), channel_id=1, source_target_pairs={{2,0},{4,2},{6,4},{8,6},{10,8},{12,10},{14,12},{16,14},{18,16},{20... | collective-permute-start | bytes 196616 | tf_op jit(solution)/shard_map/ppermute | solution.py:12
  41.2 6.4 %collective-permute-start.8 = (bf16[2,128,128]{2,1,0:T(8,128)(2,1)S(1)}, bf16[2,128,128]{2,1,0:T(8,128)(2,1)S(1)}, u32[]{:S(2)}, u32[]{:S(2)}) collective-permute-start(bf16[2,128,128]{2,1,0:T(8,128)(2,1)S(1)} %bitcast.110), channel_id=1, source_target_pairs={{30,0},{0,2},{2,4},{4,6},{6,8},{8,10},{10,12},{12,14},{14,16},{16,... | collective-permute-start | bytes 196616 | tf_op jit(solution)/shard_map/ppermute | solution.py:12
  41.7 7.3 %collective-permute-start.9 = (bf16[2,128,128]{2,1,0:T(8,128)(2,1)S(1)}, bf16[2,128,128]{2,1,0:T(8,128)(2,1)S(1)}, u32[]{:S(2)}, u32[]{:S(2)}) collective-permute-start(bf16[2,128,128]{2,1,0:T(8,128)(2,1)S(1)} %bitcast.111), channel_id=1, source_target_pairs={{28,0},{30,2},{0,4},{2,6},{4,8},{6,10},{8,12},{10,14},{12,16},{14,... | collective-permute-start | bytes 196616 | tf_op jit(solution)/shard_map/ppermute | solution.py:12
where the time goes:
time: 58.2 us; the launch traced here: 57.8 us
  starting transfers between devices  16.7 us (29%)
  matrix products  16 us (27%)
  waiting for transfers between devices  14.7 us (25%)
  local copies, waits for them, and re-layouts  7.99 us (14%)
  other arithmetic  2.16 us (4%)
    ppermute x8, starting transfers between devices, passed_along(): return lax.ppermute(block, axis, route)  12 us
    ppermute x8, waiting for transfers between devices, passed_along(): return lax.ppermute(block, axis, route)  9.82 us
    dot_general x1, matrix products, shards(): jnp.einsum('tke,tkri->eri', chosen.astype(jnp.float32), products, precisi...  5.86 us
    ppermute x1, waiting for transfers between devices, padded(): lax.ppermute(lax.slice_in_dim(block, 0, width, axis=dim), axis, backward)  4.27 us
    dot_general x1, matrix products, shards(): jnp.einsum('tro,tkio->tkri', coarse, conv_weight, preferred_element_type=...  3.85 us
    dot_general x1, matrix products, shards(): jnp.einsum('tro,tof->rtf', mixed, interp, preferred_element_type=jnp.floa...  3.46 us
    ppermute x1, starting transfers between devices, padded(): lax.ppermute(lax.slice_in_dim(block, block.shape[dim] - width, None, axis...  3.43 us
    unnamed x30, local copies, waits for them, and re-layouts  2.14 us
  transfers between devices with their start and end apart: 10, of which 8 were waited for; matrix products, arithmetic and copies ran while one was open for 2% of the time, Pallas kernels for 0%

commit v1 on v0

v1 whole, which is shorter than its diff:
```python
import functools

import jax
import jax.numpy as jnp
from jax import lax
from jax.experimental import pallas as pl
from jax.experimental.pallas import tpu as pltpu
from jax.sharding import PartitionSpec as P

MESH = pl.DeviceIdType.MESH
F32 = jnp.float32
BF16 = jnp.bfloat16


def link_offsets(reach_len):
    return [
        position - reach_len if position < reach_len else position - reach_len + 1
        for position in range(2 * reach_len)
    ]


def dot_t(left, right):
    return lax.dot_general(left, right, (((1,), (1,)), ((), ())), preferred_element_type=F32)


def kernel(
    n_patch,
    n_lev,
    fields_hbm,
    interp_hbm,
    conv_hbm,
    weight,
    send,
    pattern,
    out_hbm,
    fields,
    interp,
    conv,
    coarse,
    levels,
    middle,
    halo_out,
    halo_in,
    smooth,
    own,
    ext,
    mixed,
    out,
    which,
    slot_of,
    load_sem,
    out_sem,
    halo_sem,
    back_sem,
    forth_sem,
    *links,
):
    members, level_len, _ = fields.shape
    tiles, tile_len, fine = interp.shape
    k_len = conv_hbm.shape[1]
    link_len, most = send.shape[1], send.shape[2]
    half = (weight.shape[1] - 1) // 2
    wide = 2 * half
    rows = members * level_len
    total_levels = weight.shape[0]
    offsets = link_offsets(link_len // 2)
    returning, arrived_back, sending, arrived = (
        links[i * link_len : (i + 1) * link_len] for i in range(4)
    )
    me_p, me_l = lax.axis_index("patch"), lax.axis_index("lev")
    partner = [lax.rem(me_p + d + n_patch, n_patch) for d in offsets]
    source = [lax.rem(me_p - d + n_patch, n_patch) for d in offsets]
    order = sorted(range(link_len), key=lambda o: -abs(offsets[o]))

    load_f = pltpu.make_async_copy(fields_hbm, fields, load_sem.at[0])
    load_i = pltpu.make_async_copy(interp_hbm, interp, load_sem.at[1])
    load_c = pltpu.make_async_copy(conv_hbm, conv.at[:, pl.ds(0, k_len)], load_sem.at[2])
    load_f.start()
    load_i.start()
    load_c.start()

    barrier = pltpu.get_barrier_semaphore()
    for other in partner:
        pl.semaphore_signal(barrier, inc=1, device_id={"patch": other}, device_id_type=MESH)

    @pl.when(me_l > 0)
    def _():
        pl.semaphore_signal(barrier, inc=1, device_id={"lev": me_l - 1}, device_id_type=MESH)

    @pl.when(me_l < n_lev - 1)
    def _():
        pl.semaphore_signal(barrier, inc=1, device_id={"lev": me_l + 1}, device_id_type=MESH)

    @pl.loop(0, tiles)
    def _(t):
        named = [pattern[t, k] for k in range(k_len)]
        for e in range(tiles + link_len * most):
            index = jnp.int32(k_len)
            for k in range(k_len):
                index = jnp.where(named[k] == e, k, index)
            which[t, e] = index
        for o in range(link_len):
            index = jnp.int32(most)
            for s in range(most):
                index = jnp.where(send[0, o, s] == t, s, index)
            slot_of[t, o] = index
        conv[t, k_len] = jnp.zeros((tile_len, tile_len), BF16)

    for o in range(link_len):
        arrived_back[o][most] = jnp.zeros((rows, tile_len), BF16)
    ext[tiles] = jnp.zeros((rows, tile_len), BF16)

    load_f.wait()
    load_i.wait()
    for t in range(tiles):
        block = fields[:, :, t * fine : (t + 1) * fine].reshape(rows, fine)
        coarse[t] = dot_t(block, interp[t])
        for l in range(level_len):
            levels[wide + l, t] = coarse[t, pl.ds(l, members, stride=level_len), :]
    for i in range(wide // 2):
        low = jnp.concatenate([levels[wide + 2 * i], levels[wide + 2 * i + 1]], axis=1)
        top = level_len + 2 * i
        high = jnp.concatenate([levels[top], levels[top + 1]], axis=1)
        halo_out[0, i] = low.astype(BF16)
        halo_out[1, i] = high.astype(BF16)

    down = pltpu.make_async_remote_copy(
        halo_out.at[0],
        halo_in.at[1],
        halo_sem.at[0],
        halo_sem.at[1],
        device_id={"lev": lax.rem(me_l + n_lev - 1, n_lev)},
        device_id_type=MESH,
    )
    up = pltpu.make_async_remote_copy(
        halo_out.at[1],
        halo_in.at[0],
        halo_sem.at[2],
        halo_sem.at[3],
        device_id={"lev": lax.rem(me_l + 1, n_lev)},
        device_id_type=MESH,
    )
    beside = jnp.where(me_l > 0, 1, 0) + jnp.where(me_l < n_lev - 1, 1, 0)
    pl.semaphore_wait(barrier, link_len + beside)

    @pl.when(me_l > 0)
    def _():
        down.start()

    @pl.when(me_l < n_lev - 1)
    def _():
        up.start()

    start = me_l * level_len

    def coefficient(level, column):
        return weight[jnp.clip(start + level, 0, total_levels - 1), column]

    def adjoint_level(level):
        value = coefficient(level - half, wide) * levels[wide + level - half]
        for e in range(1 - half, half + 1):
            value = value + coefficient(level + e, half - e) * levels[wide + level + e]
        if level < 0:
            value = jnp.where(start + level >= 0, value, 0.0)
        if level >= level_len:
            value = jnp.where(start + level < total_levels, value, 0.0)
        middle[half + level] = value

    def forward_pair(level):
        both = []
        for l in (level, level + 1):
            value = coefficient(l, 0) * middle[l]
            for j in range(1, wide + 1):
                value = value + coefficient(l, j) * middle[l + j]
            both.append(value)
        smooth[:, level * members : (level + 2) * members, :] = jnp.concatenate(
            both, axis=1
        ).astype(BF16)

    for level in range(half, level_len - half):
        adjoint_level(level)
    for level in range(wide, level_len - wide, 2):
        forward_pair(level)

    def unpack(side, base):
        for i in range(wide // 2):
            pair = halo_in[side, i].astype(F32)
            levels[base + 2 * i] = pair[:, :members]
            levels[base + 2 * i + 1] = pair[:, members:]

    def clear(base):
        for i in range(wide):
            levels[base + i] = jnp.zeros(levels.shape[1:], F32)

    @pl.when(me_l > 0)
    def _():
        up.wait_recv()
        unpack(0, 0)

    @pl.when(me_l == 0)
    def _():
        clear(0)

    @pl.when(me_l < n_lev - 1)
    def _():
        down.wait_recv()
        unpack(1, wide + level_len)

    @pl.when(me_l == n_lev - 1)
    def _():
        clear(wide + level_len)

    for level in list(range(-half, half)) + list(range(level_len - half, level_len + half)):
        adjoint_level(level)
    for level in list(range(0, wide, 2)) + list(range(level_len - wide, level_len, 2)):
        forward_pair(level)

    load_c.wait()

    def gathered(first):
        left = jnp.concatenate([smooth[t] for t in range(tiles)], axis=1)
        right = jnp.concatenate(
            [
                jnp.concatenate([conv[t, which[t, first + s]] for t in range(tiles)], axis=1)
                for s in range(most)
            ],
            axis=0,
        )
        return dot_t(left, right)

    back = []
    for o in order:
        sums = gathered(tiles + o * most).astype(BF16)
        for s in range(most):
            returning[o][s] = sums[:, s * tile_len : (s + 1) * tile_len]
        copy = pltpu.make_async_remote_copy(
            returning[o],
            arrived_back[o].at[pl.ds(0, most)],
            back_sem.at[0, o],
            back_sem.at[1, o],
            device_id={"patch": source[o]},
            device_id_type=MESH,
        )
        copy.start()
        back.append(copy)
    for first in range(0, tiles, most):
        sums = gathered(first)
        for s in range(most):
            own[first + s] = sums[:, s * tile_len : (s + 1) * tile_len]
    for copy in back:
        copy.wait_recv()
    for t in range(tiles):
        value = own[t]
        for o in range(link_len):
            value = value + arrived_back[o][slot_of[t, o]].astype(F32)
        ext[t] = value.astype(BF16)
    forth = []
    for o in order:
        for s in range(most):
            sending[o][s] = ext[send[0, o, s]]
        copy = pltpu.make_async_remote_copy(
            sending[o],
            arrived[o],
            forth_sem.at[0, o],
            forth_sem.at[1, o],
            device_id={"patch": partner[o]},
            device_id_type=MESH,
        )
        copy.start()
        forth.append(copy)

    def spread(left, first, count, t):
        right = jnp.concatenate(
            [
                jnp.concatenate([conv[u, which[u, first + e]] for e in range(count)], axis=0)
                for u in (t, t + 1)
            ],
            axis=1,
        )
        return jnp.dot(left, right, preferred_element_type=F32)

    left = jnp.concatenate([ext[e] for e in range(tiles)], axis=1)
    for t in range(0, tiles, 2):
        sums = spread(left, 0, tiles, t)
        mixed[t] = sums[:, :tile_len]
        mixed[t + 1] = sums[:, tile_len:]
    near = order[::-1]
    for o in near:
        forth[order.index(o)].wait_recv()
        left = jnp.concatenate([arrived[o][s] for s in range(most)], axis=1)
        for t in range(0, tiles, 2):
            sums = spread(left, tiles + o * most, most, t)
            mixed[t] = mixed[t] + sums[:, :tile_len]
            mixed[t + 1] = mixed[t + 1] + sums[:, tile_len:]
    stores = []
    for t in range(tiles):
        part = jnp.concatenate(
            [mixed[t, pl.ds(m, level_len, stride=members), :] for m in range(members)], axis=0
        ).astype(BF16)
        result = jnp.dot(part, interp[t], preferred_element_type=F32)
        columns = pl.ds(t * fine, fine)
        out[:, :, columns] = result.reshape(members, level_len, fine)
        store = pltpu.make_async_copy(
            out.at[:, :, columns], out_hbm.at[:, :, columns], out_sem.at[t]
        )
        store.start()
        stores.append(store)
    for copy in back + forth:
        copy.wait_send()

    @pl.when(me_l > 0)
    def _():
        down.wait_send()

    @pl.when(me_l < n_lev - 1)
    def _():
        up.wait_send()

    for store in stores:
        store.wait()


def solution(mesh):
    n_patch, n_lev = mesh.shape["patch"], mesh.shape["lev"]

    def shards(fields, interp, conv_weight, vert_weight, send_tiles, tile_pattern):
        members, level_len, column_len = fields.shape
        tiles, tile_len, fine = interp.shape
        k_len = conv_weight.shape[1]
        link_len, most = send_tiles.shape[1:]
        wide = vert_weight.shape[1] - 1
        rows = members * level_len
        any_spec = pl.BlockSpec(memory_space=pl.ANY)
        smem_spec = pl.BlockSpec(memory_space=pltpu.SMEM)

        def per_link(count):
            return [pltpu.VMEM((count, rows, tile_len), BF16) for _ in range(link_len)]

        return pl.pallas_call(
            functools.partial(kernel, n_patch, n_lev),
            name="localize",
            out_shape=jax.ShapeDtypeStruct(fields.shape, F32),
            in_specs=[any_spec] * 3 + [smem_spec] * 3,
            out_specs=any_spec,
            scratch_shapes=[
                pltpu.VMEM(fields.shape, BF16),
                pltpu.VMEM(interp.shape, BF16),
                pltpu.VMEM((tiles, k_len + 1, tile_len, tile_len), BF16),
                pltpu.VMEM((tiles, rows, tile_len), F32),
                pltpu.VMEM((level_len + 2 * wide, tiles, members, tile_len), F32),
                pltpu.VMEM((level_len + wide, tiles, members, tile_len), F32),
                pltpu.VMEM((2, wide // 2, tiles, 2 * members, tile_len), BF16),
                pltpu.VMEM((2, wide // 2, tiles, 2 * members, tile_len), BF16),
                pltpu.VMEM((tiles, rows, tile_len), BF16),
                pltpu.VMEM((tiles, rows, tile_len), F32),
                pltpu.VMEM((tiles + 1, rows, tile_len), BF16),
                pltpu.VMEM((tiles, rows, tile_len), F32),
                pltpu.VMEM(fields.shape, F32),
                pltpu.SMEM((tiles, tiles + link_len * most), jnp.int32),
                pltpu.SMEM((tiles, link_len), jnp.int32),
                pltpu.SemaphoreType.DMA((3,)),
                pltpu.SemaphoreType.DMA((tiles,)),
                pltpu.SemaphoreType.DMA((4,)),
                pltpu.SemaphoreType.DMA((2, link_len)),
                pltpu.SemaphoreType.DMA((2, link_len)),
            ]
            + per_link(most)
            + per_link(most + 1)
            + per_link(most)
            + per_link(most),
            compiler_params=pltpu.CompilerParams(collective_id=0, has_side_effects=True),
        )(fields, interp, conv_weight, vert_weight, send_tiles, tile_pattern)

    in_specs = (
        P(None, "lev", "patch"),
        P("patch", None, None),
        P("patch", None, None, None),
        P(),
        P("patch", None, None),
        P("patch", None),
    )
    out_specs = P(None, "lev", "patch")
    return jax.shard_map(shards, mesh=mesh, in_specs=in_specs, out_specs=out_specs, check_vma=False)
```

time: 58.2 us -> 30 us (0.52)
  Pallas kernels: 0 us -> 24.7 us
  starting transfers between devices: 16.7 us -> 0 us
  matrix products: 16 us -> 0 us
  waiting for transfers between devices: 14.7 us -> 0 us
  local copies, waits for them, and re-layouts: 7.99 us -> 5.01 us
  other arithmetic: 2.16 us -> 0 us
    pallas_call x0 -> x1, Pallas kernels: none -> 24.7 us  [shards(): pl.pallas_call(functools.partial(kernel, n_patch, n_lev), name='localize'...]
    ppermute x10 -> x0, starting transfers between devices: 16.7 us -> none  [the longest x8 12 us: passed_along(): return lax.ppermute(block, axis, route)]
    dot_general x6 -> x0, matrix products: 16 us -> none  [the longest x1 5.86 us: shards(): jnp.einsum('tke,tkri->eri', chosen.astype(jnp.float32), products, precisi...]
    ppermute x10 -> x0, waiting for transfers between devices: 14.7 us -> none  [the longest x8 9.82 us: passed_along(): return lax.ppermute(block, axis, route)]
    unnamed x30 -> x3, local copies, waits for them, and re-layouts: 2.14 us -> 5.01 us
    transpose x1 -> x0, local copies, waits for them, and re-layouts: 1.84 us -> none  [shards(): jnp.einsum('tro,tof->rtf', mixed, interp, preferred_element_type=jnp.floa...]
    another operation x2 -> x0, other arithmetic: 1.35 us -> none  [the longest x1 1.32 us: move_links(): jnp.stack([passed_along(pieces[position], 'patch', -offsets[position]) fo...]
    mul x2 -> x0, local copies, waits for them, and re-layouts: 1.31 us -> none  [the longest x1 0.66 us: vertical_adjoint(): factor[:, None]]
  transfers between devices with their start and end apart: 10 -> 0, of which waited for: 8 -> 0; matrix products, arithmetic and copies ran while one was open for 2% -> 0% of each run, Pallas kernels for 0% -> 0%
where the time goes in v1:
time: 30 us; the launch traced here: 29.7 us
  Pallas kernels  24.7 us (82%)
  local copies, waits for them, and re-layouts  5.01 us (17%)
    pallas_call x1, Pallas kernels, shards(): pl.pallas_call(functools.partial(kernel, n_patch, n_lev), name='localize'...  24.7 us
    unnamed x3, local copies, waits for them, and re-layouts  5.01 us

profile of v1, /device:TPU:0, one launch (start us, length us, event | category | flops | bytes accessed | tf_op | source)
XLA Modules:
  0.0 29.7 jit_solution(1551093893478778882)
XLA Ops:
  0.0 1.3 %copy.8.send = s32[1,4,2]{2,1,0:T(4,128)} copy(s32[1,4,2]{1,2,0:T(2,128)} %param.10) | data formatting | bytes 64 | tf_op args[4]
  1.3 1.4 %copy.7.weight = f32[32,5]{1,0:T(8,128)} copy(f32[32,5]{0,1:T(8,128)} %param.9) | data formatting | bytes 1280 | tf_op args[3]
  2.7 24.7 %localize.1 = f32[8,16,2048]{2,1,0:T(8,128)} custom-call(bf16[8,16,2048]{2,1,0:T(8,128)(2,1)} %fields_hbm.1, bf16[8,128,256]{2,1,0:T(8,128)(2,1)} %interp_hbm.1, bf16[8,8,128,128]{3,2,1,0:T(8,128)(2,1)} %conv_hbm.1, f32[32,5]{1,0:T(8,128)} %copy.7.weight, s32[1,4,2]{2,1,0:T(4,128)} %copy.8.send, s32[8,8]{1,0:T(8,128)} %pattern.1), custom_call_target="tpu_custom_call" | custom-call | tf_op jit(solution)/shard_map/localize/pallas_call | solution.py:339
  27.4 2.3 %copy.10 = f32[8,16,2048]{2,1,0:T(8,128)} copy(f32[8,16,2048]{2,1,0:T(8,128)} %localize.1) | data formatting | bytes 2097152

commit v2 on v1

v2 whole, which is shorter than its diff:
```python
import functools

import jax
import jax.numpy as jnp
from jax import lax
from jax.experimental import pallas as pl
from jax.experimental.pallas import tpu as pltpu
from jax.sharding import PartitionSpec as P

MESH = pl.DeviceIdType.MESH
F32 = jnp.float32
BF16 = jnp.bfloat16


def link_offsets(reach_len):
    return [
        position - reach_len if position < reach_len else position - reach_len + 1
        for position in range(2 * reach_len)
    ]


def dot_t(left, right):
    return lax.dot_general(left, right, (((1,), (1,)), ((), ())), preferred_element_type=F32)


def kernel(
    n_patch,
    n_lev,
    fields_hbm,
    interp_hbm,
    conv_hbm,
    weight,
    send,
    pattern,
    out,
    fields,
    interp,
    conv,
    coarse,
    levels,
    middle,
    halo_out,
    halo_in,
    own,
    mixed,
    which,
    slot_of,
    load_sem,
    halo_sem,
    back_sem,
    forth_sem,
    *parts,
):
    members, level_len, _ = fields.shape
    tiles, tile_len, fine = interp.shape
    k_len = conv_hbm.shape[1]
    most, link_len = send.shape[1], send.shape[2]
    half = (weight.shape[0] - 1) // 2
    wide = 2 * half
    rows = members * level_len
    total_levels = weight.shape[1]
    offsets = link_offsets(link_len // 2)
    smooth, ext, links = parts[:2], parts[2:4], parts[4:]
    returning, arrived_back, sending, arrived = (
        [links[(2 * i + c) * link_len : (2 * i + c + 1) * link_len] for c in range(2)]
        for i in range(4)
    )
    edge = wide * members
    part_rows = (rows - 2 * edge, 2 * edge)
    me_p, me_l = lax.axis_index("patch"), lax.axis_index("lev")
    partner = [lax.rem(me_p + d + n_patch, n_patch) for d in offsets]
    source = [lax.rem(me_p - d + n_patch, n_patch) for d in offsets]
    order = sorted(range(link_len), key=lambda o: -abs(offsets[o]))

    load_f = pltpu.make_async_copy(fields_hbm, fields, load_sem.at[0])
    load_i = pltpu.make_async_copy(interp_hbm, interp, load_sem.at[1])
    load_c = pltpu.make_async_copy(conv_hbm, conv.at[:, pl.ds(0, k_len)], load_sem.at[2])
    load_f.start()
    load_i.start()

    barrier = pltpu.get_barrier_semaphore()
    for other in partner:
        pl.semaphore_signal(barrier, inc=1, device_id={"patch": other}, device_id_type=MESH)

    @pl.when(me_l > 0)
    def _():
        pl.semaphore_signal(barrier, inc=1, device_id={"lev": me_l - 1}, device_id_type=MESH)

    @pl.when(me_l < n_lev - 1)
    def _():
        pl.semaphore_signal(barrier, inc=1, device_id={"lev": me_l + 1}, device_id_type=MESH)

    @pl.loop(0, tiles)
    def _(t):
        named = [pattern[t, k] for k in range(k_len)]
        for e in range(tiles + link_len * most):
            index = jnp.int32(k_len)
            for k in range(k_len):
                index = jnp.where(named[k] == e, k, index)
            which[t, e] = index
        for o in range(link_len):
            index = jnp.int32(most)
            for s in range(most):
                index = jnp.where(send[0, s, o] == t, s, index)
            slot_of[t, o] = index
        conv[t, k_len] = jnp.zeros((tile_len, tile_len), BF16)

    load_c.start()
    for c in range(2):
        for o in range(link_len):
            arrived_back[c][o][most] = jnp.zeros((part_rows[c], tile_len), BF16)
        ext[c][tiles] = jnp.zeros((part_rows[c], tile_len), BF16)

    load_f.wait()
    load_i.wait()
    for t in range(tiles):
        block = fields[:, :, t * fine : (t + 1) * fine].reshape(rows, fine)
        coarse[t] = dot_t(block, interp[t])
        for l in range(level_len):
            levels[wide + l, t] = coarse[t, pl.ds(l, members, stride=level_len), :]
    for i in range(wide // 2):
        low = jnp.concatenate([levels[wide + 2 * i], levels[wide + 2 * i + 1]], axis=1)
        top = level_len + 2 * i
        high = jnp.concatenate([levels[top], levels[top + 1]], axis=1)
        halo_out[0, i] = low.astype(BF16)
        halo_out[1, i] = high.astype(BF16)

    down = pltpu.make_async_remote_copy(
        halo_out.at[0],
        halo_in.at[1],
        halo_sem.at[0],
        halo_sem.at[1],
        device_id={"lev": lax.rem(me_l + n_lev - 1, n_lev)},
        device_id_type=MESH,
    )
    up = pltpu.make_async_remote_copy(
        halo_out.at[1],
        halo_in.at[0],
        halo_sem.at[2],
        halo_sem.at[3],
        device_id={"lev": lax.rem(me_l + 1, n_lev)},
        device_id_type=MESH,
    )
    beside = jnp.where(me_l > 0, 1, 0) + jnp.where(me_l < n_lev - 1, 1, 0)
    pl.semaphore_wait(barrier, link_len + beside)

    @pl.when(me_l > 0)
    def _():
        down.start()

    @pl.when(me_l < n_lev - 1)
    def _():
        up.start()

    start = me_l * level_len

    def coefficient(level, column):
        return weight[column, jnp.clip(start + level, 0, total_levels - 1)]

    def adjoint_level(level):
        value = coefficient(level - half, wide) * levels[wide + level - half]
        for e in range(1 - half, half + 1):
            value = value + coefficient(level + e, half - e) * levels[wide + level + e]
        if level < 0:
            value = jnp.where(start + level >= 0, value, 0.0)
        if level >= level_len:
            value = jnp.where(start + level < total_levels, value, 0.0)
        middle[half + level] = value

    def forward_pair(level):
        both = []
        for l in (level, level + 1):
            value = coefficient(l, 0) * middle[l]
            for j in range(1, wide + 1):
                value = value + coefficient(l, j) * middle[l + j]
            both.append(value)
        pair = jnp.concatenate(both, axis=1).astype(BF16)
        if wide <= level < level_len - wide:
            smooth[0][:, pl.ds((level - wide) * members, 2 * members), :] = pair
        else:
            place = level if level < wide else level - level_len + 2 * wide
            smooth[1][:, pl.ds(place * members, 2 * members), :] = pair

    for level in range(half, level_len - half):
        adjoint_level(level)
    for level in range(wide, level_len - wide, 2):
        forward_pair(level)

    load_c.wait()

    def gathered(left, first):
        right = jnp.concatenate(
            [
                jnp.concatenate([conv[t, which[t, first + s]] for t in range(tiles)], axis=1)
                for s in range(most)
            ],
            axis=0,
        )
        return dot_t(left, right)

    def side_by_side(ref, count):
        return jnp.concatenate([ref[i] for i in range(count)], axis=1)

    def send_back(c):
        left = side_by_side(smooth[c], tiles)
        copies = {}
        for o in order:
            sums = gathered(left, tiles + o * most).astype(BF16)
            for s in range(most):
                returning[c][o][s] = sums[:, s * tile_len : (s + 1) * tile_len]
            copies[o] = pltpu.make_async_remote_copy(
                returning[c][o],
                arrived_back[c][o].at[pl.ds(0, most)],
                back_sem.at[0, c, o],
                back_sem.at[1, c, o],
                device_id={"patch": source[o]},
                device_id_type=MESH,
            )
            copies[o].start()
        return copies

    def send_forth(c):
        low = 0 if c == 0 else part_rows[0]
        for t in range(tiles):
            value = own[t, low : low + part_rows[c]]
            for o in range(link_len):
                value = value + arrived_back[c][o][slot_of[t, o]].astype(F32)
            ext[c][t] = value.astype(BF16)
        copies = {}
        for o in order:
            for s in range(most):
                sending[c][o][s] = ext[c][send[0, s, o]]
            copies[o] = pltpu.make_async_remote_copy(
                sending[c][o],
                arrived[c][o],
                forth_sem.at[0, c, o],
                forth_sem.at[1, c, o],
                device_id={"patch": partner[o]},
                device_id_type=MESH,
            )
            copies[o].start()
        return copies

    def spread(left, first, count, t):
        right = jnp.concatenate(
            [
                jnp.concatenate([conv[u, which[u, first + e]] for e in range(count)], axis=0)
                for u in (t, t + 1)
            ],
            axis=1,
        )
        return jnp.dot(left, right, preferred_element_type=F32)

    def places(c):
        if c == 0:
            return [(0, part_rows[0], edge)]
        return [(0, edge, 0), (edge, edge, rows - edge)]

    def put(c, t, sums, fresh):
        for begin, count, place in places(c):
            for i in range(2):
                value = sums[begin : begin + count, i * tile_len : (i + 1) * tile_len]
                if not fresh:
                    value = value + mixed[t + i, pl.ds(place, count)]
                mixed[t + i, pl.ds(place, count)] = value

    def mix_own(c):
        left = side_by_side(ext[c], tiles)
        for t in range(0, tiles, 2):
            put(c, t, spread(left, 0, tiles, t), True)

    def mix_link(c, o):
        left = side_by_side(arrived[c][o], most)
        for t in range(0, tiles, 2):
            put(c, t, spread(left, tiles + o * most, most, t), False)

    back = [send_back(0)]

    def unpack(side, base):
        for i in range(wide // 2):
            pair = halo_in[side, i].astype(F32)
            levels[base + 2 * i] = pair[:, :members]
            levels[base + 2 * i + 1] = pair[:, members:]

    def clear(base):
        for i in range(wide):
            levels[base + i] = jnp.zeros(levels.shape[1:], F32)

    @pl.when(me_l > 0)
    def _():
        up.wait_recv()
        unpack(0, 0)

    @pl.when(me_l == 0)
    def _():
        clear(0)

    @pl.when(me_l < n_lev - 1)
    def _():
        down.wait_recv()
        unpack(1, wide + level_len)

    @pl.when(me_l == n_lev - 1)
    def _():
        clear(wide + level_len)

    for level in list(range(-half, half)) + list(range(level_len - half, level_len + half)):
        adjoint_level(level)
    for level in list(range(0, wide, 2)) + list(range(level_len - wide, level_len, 2)):
        forward_pair(level)

    back.append(send_back(1))
    left = jnp.concatenate([side_by_side(smooth[c], tiles) for c in range(2)], axis=0)
    for first in range(0, tiles, most):
        sums = gathered(left, first)
        for s in range(most):
            own[first + s] = sums[:, s * tile_len : (s + 1) * tile_len]
    forth = []
    for c in range(2):
        for o in order:
            back[c][o].wait_recv()
        forth.append(send_forth(c))
        mix_own(c)
    for c in range(2):
        for o in order[::-1]:
            forth[c][o].wait_recv()
            mix_link(c, o)
    for t in range(tiles):
        part = jnp.concatenate(
            [mixed[t, pl.ds(m, level_len, stride=members), :] for m in range(members)], axis=0
        ).astype(BF16)
        result = jnp.dot(part, interp[t], preferred_element_type=F32)
        out[:, :, t * fine : (t + 1) * fine] = result.reshape(members, level_len, fine)
    for copies in back + forth:
        for o in order:
            copies[o].wait_send()

    @pl.when(me_l > 0)
    def _():
        down.wait_send()

    @pl.when(me_l < n_lev - 1)
    def _():
        up.wait_send()


def solution(mesh):
    n_patch, n_lev = mesh.shape["patch"], mesh.shape["lev"]

    def shards(fields, interp, conv_weight, vert_weight, send_tiles, tile_pattern):
        members, level_len, column_len = fields.shape
        tiles, tile_len, fine = interp.shape
        k_len = conv_weight.shape[1]
        link_len, most = send_tiles.shape[1:]
        wide = vert_weight.shape[1] - 1
        rows = members * level_len
        any_spec = pl.BlockSpec(memory_space=pl.ANY)
        smem_spec = pl.BlockSpec(memory_space=pltpu.SMEM)

        edge = 2 * wide * members

        def per_part(count, copies):
            return [
                pltpu.VMEM((count, part_rows, tile_len), BF16)
                for part_rows in (rows - edge, edge)
                for _ in range(copies)
            ]

        return pl.pallas_call(
            functools.partial(kernel, n_patch, n_lev),
            name="localize",
            out_shape=pltpu.VMEM(fields.shape, F32),
            in_specs=[any_spec] * 3 + [smem_spec] * 3,
            out_specs=pl.BlockSpec(memory_space=pltpu.VMEM),
            scratch_shapes=[
                pltpu.VMEM(fields.shape, BF16),
                pltpu.VMEM(interp.shape, BF16),
                pltpu.VMEM((tiles, k_len + 1, tile_len, tile_len), BF16),
                pltpu.VMEM((tiles, rows, tile_len), F32),
                pltpu.VMEM((level_len + 2 * wide, tiles, members, tile_len), F32),
                pltpu.VMEM((level_len + wide, tiles, members, tile_len), F32),
                pltpu.VMEM((2, wide // 2, tiles, 2 * members, tile_len), BF16),
                pltpu.VMEM((2, wide // 2, tiles, 2 * members, tile_len), BF16),
                pltpu.VMEM((tiles, rows, tile_len), F32),
                pltpu.VMEM((tiles, rows, tile_len), F32),
                pltpu.SMEM((tiles, tiles + link_len * most), jnp.int32),
                pltpu.SMEM((tiles, link_len), jnp.int32),
                pltpu.SemaphoreType.DMA((3,)),
                pltpu.SemaphoreType.DMA((4,)),
                pltpu.SemaphoreType.DMA((2, 2, link_len)),
                pltpu.SemaphoreType.DMA((2, 2, link_len)),
            ]
            + per_part(tiles, 1)
            + per_part(tiles + 1, 1)
            + per_part(most, link_len)
            + per_part(most + 1, link_len)
            + per_part(most, link_len)
            + per_part(most, link_len),
            compiler_params=pltpu.CompilerParams(collective_id=0, has_side_effects=True),
        )(fields, interp, conv_weight, vert_weight.T, send_tiles.transpose(0, 2, 1), tile_pattern)

    in_specs = (
        P(None, "lev", "patch"),
        P("patch", None, None),
        P("patch", None, None, None),
        P(),
        P("patch", None, None),
        P("patch", None),
    )
    out_specs = P(None, "lev", "patch")
    return jax.shard_map(shards, mesh=mesh, in_specs=in_specs, out_specs=out_specs, check_vma=False)
```

time: 30 us -> 23 us (0.77)
  local copies, waits for them, and re-layouts: 5.01 us -> 0.97 us
  Pallas kernels: 24.7 us -> 21.9 us
    unnamed x3 -> x1, local copies, waits for them, and re-layouts: 5.01 us -> 0.97 us
    pallas_call x1, Pallas kernels: 24.7 us -> 21.9 us  [shards(): pl.pallas_call(functools.partial(kernel, n_patch, n_lev), name='localize'...]
where the time goes in v2:
time: 23 us; the launch traced here: 22.9 us
  Pallas kernels  21.9 us (95%)
  local copies, waits for them, and re-layouts  0.97 us (4%)
    pallas_call x1, Pallas kernels, shards(): pl.pallas_call(functools.partial(kernel, n_patch, n_lev), name='localize'...  21.9 us
    unnamed x1, local copies, waits for them, and re-layouts  0.97 us

profile of v2, /device:TPU:0, one launch (start us, length us, event | category | flops | bytes accessed | tf_op | source)
XLA Modules:
  0.0 22.9 jit_solution(6205912854543792771)
XLA Ops:
  0.0 21.9 %localize.1 = f32[8,16,2048]{2,1,0:T(8,128)S(1)} custom-call(bf16[8,16,2048]{2,1,0:T(8,128)(2,1)} %fields_hbm.1, bf16[8,128,256]{2,1,0:T(8,128)(2,1)} %interp_hbm.1, bf16[8,8,128,128]{3,2,1,0:T(8,128)(2,1)} %conv_hbm.1, f32[5,32]{1,0:T(8,128)} %bitcast.2, s32[1,2,4]{2,1,0:T(2,128)} %bitcast.3, s32[8,8]{1,0:T(8,128)} %pattern.1), custom_call_target="tpu_custom_call" | custom-call | tf_op jit(solution)/shard_map/localize/pallas_call | solution.py:369
  21.9 1.0 %copy.8 = f32[8,16,2048]{2,1,0:T(8,128)} copy(f32[8,16,2048]{2,1,0:T(8,128)S(1)} %localize.1) | data formatting | bytes 2097152

commit v3 on v2

--- a/solution.py
+++ b/solution.py
@@ -141,17 +141,6 @@
         device_id={"lev": lax.rem(me_l + 1, n_lev)},
         device_id_type=MESH,
     )
-    beside = jnp.where(me_l > 0, 1, 0) + jnp.where(me_l < n_lev - 1, 1, 0)
-    pl.semaphore_wait(barrier, link_len + beside)
-
-    @pl.when(me_l > 0)
-    def _():
-        down.start()
-
-    @pl.when(me_l < n_lev - 1)
-    def _():
-        up.start()
-
     start = me_l * level_len
 
     def coefficient(level, column):
@@ -201,23 +190,32 @@
     def side_by_side(ref, count):
         return jnp.concatenate([ref[i] for i in range(count)], axis=1)
 
-    def send_back(c):
+    def sum_back(c, o):
+        sums = gathered(side_by_side(smooth[c], tiles), tiles + o * most).astype(BF16)
+        for s in range(most):
+            returning[c][o][s] = sums[:, s * tile_len : (s + 1) * tile_len]
+
+    def send_back(c, o):
+        copy = pltpu.make_async_remote_copy(
+            returning[c][o],
+            arrived_back[c][o].at[pl.ds(0, most)],
+            back_sem.at[0, c, o],
+            back_sem.at[1, c, o],
+            device_id={"patch": source[o]},
+            device_id_type=MESH,
+        )
+        copy.start()
+        return copy
+
+    def sum_own(c):
+        low = 0 if c == 0 else part_rows[0]
         left = side_by_side(smooth[c], tiles)
-        copies = {}
-        for o in order:
-            sums = gathered(left, tiles + o * most).astype(BF16)
+        for first in range(0, tiles, most):
+            sums = gathered(left, first)
             for s in range(most):
-                returning[c][o][s] = sums[:, s * tile_len : (s + 1) * tile_len]
-            copies[o] = pltpu.make_async_remote_copy(
-                returning[c][o],
-                arrived_back[c][o].at[pl.ds(0, most)],
-                back_sem.at[0, c, o],
-                back_sem.at[1, c, o],
-                device_id={"patch": source[o]},
-                device_id_type=MESH,
-            )
-            copies[o].start()
-        return copies
+                own[first + s, pl.ds(low, part_rows[c])] = sums[
+                    :, s * tile_len : (s + 1) * tile_len
+                ]
 
     def send_forth(c):
         low = 0 if c == 0 else part_rows[0]
@@ -274,7 +272,21 @@
         for t in range(0, tiles, 2):
             put(c, t, spread(left, tiles + o * most, most, t), False)
 
-    back = [send_back(0)]
+    for o in order:
+        sum_back(0, o)
+    beside = jnp.where(me_l > 0, 1, 0) + jnp.where(me_l < n_lev - 1, 1, 0)
+    pl.semaphore_wait(barrier, link_len + beside)
+
+    @pl.when(me_l > 0)
+    def _():
+        down.start()
+
+    @pl.when(me_l < n_lev - 1)
+    def _():
+        up.start()
+
+    back = [{o: send_back(0, o) for o in order}, {}]
+    sum_own(0)
 
     def unpack(side, base):
         for i in range(wide // 2):
@@ -309,12 +321,10 @@
     for level in list(range(0, wide, 2)) + list(range(level_len - wide, level_len, 2)):
         forward_pair(level)
 
-    back.append(send_back(1))
-    left = jnp.concatenate([side_by_side(smooth[c], tiles) for c in range(2)], axis=0)
-    for first in range(0, tiles, most):
-        sums = gathered(left, first)
-        for s in range(most):
-            own[first + s] = sums[:, s * tile_len : (s + 1) * tile_len]
+    for o in order:
+        sum_back(1, o)
+        back[1][o] = send_back(1, o)
+    sum_own(1)
     forth = []
     for c in range(2):
         for o in order:

time: 23 us -> 23 us (level)
  no operation moved by 1% of the time
where the time goes in v3:
time: 23 us; the launch traced here: 22.8 us
  Pallas kernels  21.8 us (95%)
  local copies, waits for them, and re-layouts  0.97 us (4%)
    pallas_call x1, Pallas kernels, shards(): pl.pallas_call(functools.partial(kernel, n_patch, n_lev), name='localize'...  21.8 us
    unnamed x1, local copies, waits for them, and re-layouts  0.97 us

profile of v3, /device:TPU:0, one launch (start us, length us, event | category | flops | bytes accessed | tf_op | source)
XLA Modules:
  0.0 22.8 jit_solution(4238844695878587356)
XLA Ops:
  0.0 21.8 %localize.1 = f32[8,16,2048]{2,1,0:T(8,128)S(1)} custom-call(bf16[8,16,2048]{2,1,0:T(8,128)(2,1)} %fields_hbm.1, bf16[8,128,256]{2,1,0:T(8,128)(2,1)} %interp_hbm.1, bf16[8,8,128,128]{3,2,1,0:T(8,128)(2,1)} %conv_hbm.1, f32[5,32]{1,0:T(8,128)} %bitcast.2, s32[1,2,4]{2,1,0:T(2,128)} %bitcast.3, s32[8,8]{1,0:T(8,128)} %pattern.1), custom_call_target="tpu_custom_call" | custom-call | tf_op jit(solution)/shard_map/localize/pallas_call | solution.py:379
  21.8 1.0 %copy.8 = f32[8,16,2048]{2,1,0:T(8,128)} copy(f32[8,16,2048]{2,1,0:T(8,128)S(1)} %localize.1) | data formatting | bytes 2097152
